TPU v7x, 32 devices: a whole 2x2x4 slice. The times are simulated.
32 devices in a mesh: grp: 4 (over x, core), sub: 8 (over z, y).
Axes of the slice: x: 2, y: 2, z: 4, core: 2. Of those that a mesh axis runs over, the one named last changes fastest.
Arguments:
- fine_res: float32 [3, 131072], P(None, ('grp', 'sub'))
- node_map: int32 [2, 131072], P(None, ('grp', 'sub')), may hold values from 0 to 16383, as said below
- connect: int32 [4, 32768], P(None, 'sub'), may hold values from 0 to 16383, as said below
- grads: float32 [3, 3, 32768], P(None, None, 'sub'), may hold values from -6 to 6
- moduli: float32 [2, 32768], P(None, 'sub'), may hold values from 0.2 to 2
- mass: float32 [16384], P('sub'), may hold values from 0.5 to 4
Outputs:
- correction: float32 [3, 131072], P(None, ('grp', 'sub'))
Inputs may be any that keep to these rules, and one draw needn't show every extreme that they name: `node_map`: fine nodes 4096 * b to 4096 * (b + 1) - 1 lie in column c = b % 8; both their entries are coarse nodes c * 2048 to (c + 1) * 2048 - 1 or the first 1024 nodes of column c + 1; the two entries are equal at vertices. `connect`: tetrahedra c * 4096 to (c + 1) * 4096 - 1 lie in column c; their nodes are coarse nodes of column c or the first 1024 nodes of column c + 1.
All inputs are finite; a program needn't handle non-finite values.
Results may differ from a plain program's by a relative error of at most 0.0001.
Values sent between devices are 32-bit elements; how exact they have to be, the bound alone decides.
No kernel may reach another device: no remote copies, remote signals or barrier semaphores. Data moves between devices by JAX's collectives and lax.ppermute only.
A program may use at most 64 MiB of HBM per device.

v0:
```python
import jax
import jax.numpy as jnp
from jax import lax
from jax.sharding import PartitionSpec as P

CN = 2048
CI = 1024
CE = 4096
ITERS = 3


def shifted(shard, axis, by):
    size = lax.axis_size(axis)
    pairs = [(i, i + by) for i in range(size) if 0 <= i + by < size]
    return lax.ppermute(shard, axis, pairs)


def element_forces(field, connect, grads, moduli, count):
    last = -(grads[:, 0] + grads[:, 1] + grads[:, 2])
    shape_grads = (grads[:, 0], grads[:, 1], grads[:, 2], last)
    displ_grad = jnp.zeros((3, 3, connect.shape[1]), jnp.float32)
    for corner in range(4):
        moved = jnp.take(field, connect[corner], axis=1)
        displ_grad = displ_grad + moved[:, None, :] * shape_grads[corner][None, :, :]
    strain = 0.5 * (displ_grad + jnp.transpose(displ_grad, (1, 0, 2)))
    trace = strain[0, 0] + strain[1, 1] + strain[2, 2]
    identity = jnp.eye(3, dtype=jnp.float32)[:, :, None]
    stress = 2.0 * moduli[1] * strain + moduli[0] * trace * identity
    forces = jnp.zeros((3, count), jnp.float32)
    for corner in range(4):
        nodal = jnp.sum(stress * shape_grads[corner][None, :, :], axis=1)
        forces = forces.at[:, connect[corner]].add(nodal)
    return forces


def squares(residual):
    return lax.psum(jnp.sum(residual * residual), "sub")


def body(fine_res, node_map, connect, grads, moduli, mass):
    column = lax.axis_index("sub")
    offset = column * CN
    local_map = node_map - offset
    local_conn = connect - offset
    span = CN + CI
    share = CE // lax.axis_size("grp")
    start = lax.axis_index("grp") * share
    local_conn = lax.dynamic_slice_in_dim(local_conn, start, share, 1)
    grads = lax.dynamic_slice_in_dim(grads, start, share, 2)
    moduli = lax.dynamic_slice_in_dim(moduli, start, share, 1)
    half = 0.5 * fine_res
    partial_rhs = (
        jnp.zeros((3, span), jnp.float32)
        .at[:, local_map[0]]
        .add(half)
        .at[:, local_map[1]]
        .add(half)
    )
    column_rhs = lax.psum(partial_rhs, "grp")
    carried = shifted(column_rhs[:, CN:], "sub", 1)
    rhs = column_rhs[:, :CN].at[:, :CI].add(carried)
    solution = jnp.zeros(rhs.shape, jnp.float32)
    residual = rhs
    direction = rhs
    norm_now = squares(residual)
    for step in range(ITERS):
        operate_upper = shifted(direction[:, :CI], "sub", -1)
        operate_extended = jnp.concatenate([direction, operate_upper], axis=1)
        forces = element_forces(operate_extended, local_conn, grads, moduli, span)
        forces = lax.psum(forces, "grp")
        returned = shifted(forces[:, CN:], "sub", 1)
        own = forces[:, :CN] + mass[None, :] * direction
        image = own.at[:, :CI].add(returned)
        curv = jnp.sum(direction * image)
        alpha = norm_now / lax.psum(curv, "sub")
        solution = solution + alpha * direction
        residual = residual - alpha * image
        if step + 1 < ITERS:
            norm_next = squares(residual)
            direction = residual + norm_next / norm_now * direction
            norm_now = norm_next
    upper = shifted(solution[:, :CI], "sub", -1)
    extended = jnp.concatenate([solution, upper], axis=1)
    return 0.5 * (
        jnp.take(extended, local_map[0], axis=1) + jnp.take(extended, local_map[1], axis=1)
    )


def solution(mesh):
    in_specs = (
        P(None, ("grp", "sub")),
        P(None, ("grp", "sub")),
        P(None, "sub"),
        P(None, None, "sub"),
        P(None, "sub"),
        P("sub"),
    )
    out_specs = P(None, ("grp", "sub"))
    return jax.shard_map(body, mesh=mesh, in_specs=in_specs, out_specs=out_specs, check_vma=False)
```

profile of v0, /device:TPU:0, one launch (start us, length us, event | category | flops | bytes accessed | tf_op | source)
XLA Modules:
  0.0 632.5 jit_solution(18020449593061128261)
XLA Ops:
  2.3 23.6 %scatter_custom_fusion = f32[3,3072]{0,1:T(8,128)} fusion(s32[4096]{0:T(1024)S(1)} %bitcast.139, f32[4096,3]{1,0:T(8,128)S(1)} %copy.154, f32[]{:T(128)} %constant.127.clone.1), kind=kCustom, calls=%fused_computation.56 | custom fusion | flops 12288 | bytes 36868 | tf_op jit(solution)/shard_map/scatter-add | solution.py:55
  25.9 22.7 %scatter_fusion = f32[3,3072]{0,1:T(8,128)} fusion(f32[3,3072]{0,1:T(8,128)} %scatter_custom_fusion, s32[4096]{0:T(1024)S(1)} %bitcast.112, f32[4096,3]{1,0:T(8,128)S(1)} %copy.154), kind=kCustom, calls=%fused_computation.15 | custom fusion | flops 12288 | bytes 163840 | tf_op jit(solution)/shard_map/scatter-add | solution.py:57
  48.5 34.5 %psum.70 = f32[3,3072]{0,1:T(8,128)S(1)} all-reduce(f32[3,3072]{0,1:T(8,128)} %scatter_fusion), channel_id=1, replica_groups=mesh['grp'=4,'sub'=8] {'grp'}, use_global_device_ids=true, to_apply=%region_2.0 | all-reduce | flops 9216 | bytes 73728 | tf_op jit(solution)/shard_map/psum | solution.py:59
  90.0 9.4 %collective-permute-done = f32[3,1024]{0,1:T(8,128)S(1)} collective-permute-done((f32[3,1024]{0,1:T(8,128)}, f32[3,1024]{0,1:T(8,128)S(1)}, u32[]{:S(2)}, u32[]{:S(2)}) %collective-permute-start) | collective-permute-done | bytes 12320 | tf_op jit(solution)/shard_map/ppermute | solution.py:15
  101.5 14.5 %collective-permute-done.1 = f32[3,1024]{0,1:T(8,128)S(1)} collective-permute-done((f32[3,1024]{0,1:T(8,128)S(1)}, f32[3,1024]{0,1:T(8,128)S(1)}, u32[]{:S(2)}, u32[]{:S(2)}) %collective-permute-start.1) | collective-permute-done | bytes 12320 | tf_op jit(solution)/shard_map/ppermute | solution.py:15
  139.3 6.8 %scatter_custom_fusion.2 = f32[3,3072]{0,1:T(8,128)S(1)} fusion(s32[1024]{0:T(1024)S(1)} %bitcast.140, f32[1024,3]{1,0:T(8,128)} %copy.165, f32[]{:T(128)} %constant.127.clone.1), kind=kCustom, calls=%fused_computation.54 | custom fusion | flops 3072 | bytes 37376 | tf_op jit(solution)/shard_map/scatter-add | solution.py:32
  146.1 7.0 %scatter_fusion.1 = f32[3,3072]{0,1:T(8,128)S(1)} fusion(f32[3,3072]{0,1:T(8,128)S(1)} %scatter_custom_fusion.2, s32[1024]{0:T(1024)S(1)} %bitcast.109, f32[1024,3]{1,0:T(8,128)} %copy.166), kind=kCustom, calls=%fused_computation.17 | custom fusion | flops 3072 | bytes 40960 | tf_op jit(solution)/shard_map/scatter-add | solution.py:32
  153.1 7.5 %scatter_fusion.2 = f32[3,3072]{0,1:T(8,128)S(1)} fusion(f32[3,3072]{0,1:T(8,128)S(1)} %scatter_fusion.1, s32[1024]{0:T(1024)S(1)} %bitcast.106, f32[1024,3]{1,0:T(8,128)} %copy.167), kind=kCustom, calls=%fused_computation.18 | custom fusion | flops 3072 | bytes 40960 | tf_op jit(solution)/shard_map/scatter-add | solution.py:32
  167.2 32.0 %psum.72 = f32[3,3072]{0,1:T(8,128)} all-reduce(f32[3,3072]{0,1:T(8,128)S(1)} %scatter_fusion.3), channel_id=1, replica_groups=mesh['grp'=4,'sub'=8] {'grp'}, use_global_device_ids=true, to_apply=%region_14.16 | all-reduce | flops 9216 | bytes 73728 | tf_op jit(solution)/shard_map/psum | solution.py:70
  206.2 10.0 %collective-permute-done.2 = f32[3,1024]{0,1:T(8,128)S(1)} collective-permute-done((f32[3,1024]{0,1:T(8,128)S(1)}, f32[3,1024]{0,1:T(8,128)S(1)}, u32[]{:S(2)}, u32[]{:S(2)}) %collective-permute-start.2) | collective-permute-done | bytes 12320 | tf_op jit(solution)/shard_map/ppermute | solution.py:15
  217.9 22.1 %all-reduce = (f32[]{:T(128)}, f32[]{:T(128)}) all-reduce(f32[]{:T(128)} %get-tuple-element.56, f32[]{:T(128)} %get-tuple-element.55), channel_id=1, replica_groups=mesh['grp'=4,'sub'=8] {'sub'}, use_global_device_ids=true, to_apply=%region_5.0 | all-reduce | flops 2 | bytes 16 | tf_op jit(solution)/shard_map/psum | solution.py:37
  242.3 17.9 %psum.74 = f32[]{:T(128)} all-reduce(f32[]{:T(128)} %get-tuple-element.75), channel_id=1, replica_groups=mesh['grp'=4,'sub'=8] {'sub'}, use_global_device_ids=true, to_apply=%region_18.20 | all-reduce | flops 1 | bytes 8 | tf_op jit(solution)/shard_map/psum | solution.py:37
  263.0 10.1 %collective-permute-done.3 = f32[3,1024]{0,1:T(8,128)S(1)} collective-permute-done((f32[3,1024]{0,1:T(8,128)S(1)}, f32[3,1024]{0,1:T(8,128)S(1)}, u32[]{:S(2)}, u32[]{:S(2)}) %collective-permute-start.3) | collective-permute-done | bytes 12320 | tf_op jit(solution)/shard_map/ppermute | solution.py:15
  300.0 7.4 %scatter_custom_fusion.6 = f32[3,3072]{0,1:T(8,128)} fusion(s32[1024]{0:T(1024)S(1)} %bitcast.141, f32[1024,3]{1,0:T(8,128)S(1)} %copy.177, f32[]{:T(128)} %constant.127.clone.1), kind=kCustom, calls=%fused_computation.52 | custom fusion | flops 3072 | bytes 36868 | tf_op jit(solution)/shard_map/scatter-add | solution.py:32
  308.9 8.0 %scatter_fusion.4 = f32[3,3072]{0,1:T(8,128)} fusion(f32[3,3072]{0,1:T(8,128)} %scatter_custom_fusion.6, s32[1024]{0:T(1024)S(1)} %bitcast.110, f32[1024,3]{1,0:T(8,128)S(1)} %copy.178), kind=kCustom, calls=%fused_computation.21 | custom fusion | flops 3072 | bytes 40960 | tf_op jit(solution)/shard_map/scatter-add | solution.py:32
  316.9 8.0 %scatter_fusion.5 = f32[3,3072]{0,1:T(8,128)} fusion(f32[3,3072]{0,1:T(8,128)} %scatter_fusion.4, s32[1024]{0:T(1024)S(1)} %bitcast.107, f32[1024,3]{1,0:T(8,128)S(1)} %copy.179), kind=kCustom, calls=%fused_computation.22 | custom fusion | flops 3072 | bytes 40960 | tf_op jit(solution)/shard_map/scatter-add | solution.py:32
  324.8 8.4 %scatter_fusion.6 = f32[3,3072]{0,1:T(8,128)} fusion(f32[3,3072]{0,1:T(8,128)} %scatter_fusion.5, s32[1024]{0:T(1024)S(1)} %bitcast.104, f32[1024,3]{1,0:T(8,128)} %copy.180), kind=kCustom, calls=%fused_computation.23 | custom fusion | flops 3072 | bytes 40960 | tf_op jit(solution)/shard_map/scatter-add | solution.py:32
  333.2 32.8 %psum.75 = f32[3,3072]{0,1:T(8,128)} all-reduce(f32[3,3072]{0,1:T(8,128)} %scatter_fusion.6), channel_id=1, replica_groups=mesh['grp'=4,'sub'=8] {'grp'}, use_global_device_ids=true, to_apply=%region_27.29 | all-reduce | flops 9216 | bytes 73728 | tf_op jit(solution)/shard_map/psum | solution.py:70
  373.5 10.0 %collective-permute-done.4 = f32[3,1024]{0,1:T(8,128)S(1)} collective-permute-done((f32[3,1024]{0,1:T(8,128)S(1)}, f32[3,1024]{0,1:T(8,128)S(1)}, u32[]{:S(2)}, u32[]{:S(2)}) %collective-permute-start.4) | collective-permute-done | bytes 12320 | tf_op jit(solution)/shard_map/ppermute | solution.py:15
  385.2 20.3 %psum.76 = f32[]{:T(128)} all-reduce(f32[]{:T(128)} %multiply_reduce_fusion.2), channel_id=1, replica_groups=mesh['grp'=4,'sub'=8] {'sub'}, use_global_device_ids=true, to_apply=%region_29.31 | all-reduce | flops 1 | bytes 8 | tf_op jit(solution)/shard_map/psum | solution.py:75
  409.0 17.7 %psum.77 = f32[]{:T(128)} all-reduce(f32[]{:T(128)} %multiply_reduce_fusion.1), channel_id=1, replica_groups=mesh['grp'=4,'sub'=8] {'sub'}, use_global_device_ids=true, to_apply=%region_31.33 | all-reduce | flops 1 | bytes 8 | tf_op jit(solution)/shard_map/psum | solution.py:37
  431.2 9.5 %collective-permute-done.5 = f32[3,1024]{0,1:T(8,128)S(1)} collective-permute-done((f32[3,1024]{0,1:T(8,128)S(1)}, f32[3,1024]{0,1:T(8,128)S(1)}, u32[]{:S(2)}, u32[]{:S(2)}) %collective-permute-start.5) | collective-permute-done | bytes 12320 | tf_op jit(solution)/shard_map/ppermute | solution.py:15
  478.1 7.6 %scatter_custom_fusion.10 = f32[3,3072]{0,1:T(8,128)} fusion(s32[1024]{0:T(1024)S(1)} %bitcast.142, f32[1024,3]{1,0:T(8,128)} %copy.189, f32[]{:T(128)} %constant.127.clone.1), kind=kCustom, calls=%fused_computation.50 | custom fusion | flops 3072 | bytes 37376 | tf_op jit(solution)/shard_map/scatter-add | solution.py:32
  488.8 8.4 %scatter_fusion.7 = f32[3,3072]{0,1:T(8,128)} fusion(f32[3,3072]{0,1:T(8,128)} %scatter_custom_fusion.10, s32[1024]{0:T(1024)S(1)} %bitcast.111, f32[1024,3]{1,0:T(8,128)} %copy.190), kind=kCustom, calls=%fused_computation.25 | custom fusion | flops 3072 | bytes 40960 | tf_op jit(solution)/shard_map/scatter-add | solution.py:32
  497.2 8.4 %scatter_fusion.8 = f32[3,3072]{0,1:T(8,128)} fusion(f32[3,3072]{0,1:T(8,128)} %scatter_fusion.7, s32[1024]{0:T(1024)S(1)} %bitcast.108, f32[1024,3]{1,0:T(8,128)} %copy.191), kind=kCustom, calls=%fused_computation.26 | custom fusion | flops 3072 | bytes 40960 | tf_op jit(solution)/shard_map/scatter-add | solution.py:32
  505.5 8.4 %scatter_fusion.9 = f32[3,3072]{0,1:T(8,128)} fusion(f32[3,3072]{0,1:T(8,128)} %scatter_fusion.8, s32[1024]{0:T(1024)S(1)} %bitcast.105, f32[1024,3]{1,0:T(8,128)} %copy.192), kind=kCustom, calls=%fused_computation.27 | custom fusion | flops 3072 | bytes 40960 | tf_op jit(solution)/shard_map/scatter-add | solution.py:32
  513.9 32.9 %psum.78 = f32[3,3072]{0,1:T(8,128)} all-reduce(f32[3,3072]{0,1:T(8,128)} %scatter_fusion.9), channel_id=1, replica_groups=mesh['grp'=4,'sub'=8] {'grp'}, use_global_device_ids=true, to_apply=%region_40.42 | all-reduce | flops 9216 | bytes 73728 | tf_op jit(solution)/shard_map/psum | solution.py:70
  554.3 9.9 %collective-permute-done.6 = f32[3,1024]{0,1:T(8,128)S(1)} collective-permute-done((f32[3,1024]{0,1:T(8,128)S(1)}, f32[3,1024]{0,1:T(8,128)S(1)}, u32[]{:S(2)}, u32[]{:S(2)}) %collective-permute-start.6) | collective-permute-done | bytes 12320 | tf_op jit(solution)/shard_map/ppermute | solution.py:15
  565.9 20.2 %psum.79 = f32[]{:T(128)} all-reduce(f32[]{:T(128)} %multiply_reduce_fusion), channel_id=1, replica_groups=mesh['grp'=4,'sub'=8] {'sub'}, use_global_device_ids=true, to_apply=%region_42.44 | all-reduce | flops 1 | bytes 8 | tf_op jit(solution)/shard_map/psum | solution.py:75
  588.9 9.9 %collective-permute-done.7 = f32[3,1024]{0,1:T(8,128)S(1)} collective-permute-done((f32[3,1024]{0,1:T(8,128)S(1)}, f32[3,1024]{0,1:T(8,128)S(1)}, u32[]{:S(2)}, u32[]{:S(2)}) %collective-permute-start.7) | collective-permute-done | bytes 12320 | tf_op jit(solution)/shard_map/ppermute | solution.py:15
  599.0 14.1 %gather_fusion.12 = f32[4096,3]{1,0:T(8,128)} fusion(f32[3,3072]{0,1:T(8,128)S(1)} %pad_maximum_fusion.3, s32[4096]{0:T(1024)S(1)} %fusion.12), kind=kCustom, calls=%fused_computation.1.clone | custom fusion | bytes 114688 | tf_op jit(solution)/shard_map/jit(_take)/gather | solution.py:85
  615.3 14.1 %gather_fusion.13 = f32[4096,3]{1,0:T(8,128)} fusion(f32[3,3072]{0,1:T(8,128)S(1)} %pad_maximum_fusion.3, s32[4096]{0:T(1024)S(1)} %fusion.13), kind=kCustom, calls=%fused_computation.13.clone | custom fusion | bytes 114688 | tf_op jit(solution)/shard_map/jit(_take)/gather | solution.py:85
  (126 shorter events, 151.4 us)
Async XLA Ops:
  83.9 15.5 %collective-permute-start = (f32[3,1024]{0,1:T(8,128)}, f32[3,1024]{0,1:T(8,128)S(1)}, u32[]{:S(2)}, u32[]{:S(2)}) collective-permute-start(f32[3,1024]{0,1:T(8,128)} %slice.282), channel_id=1, source_target_pairs={{0,1},{1,2},{2,3},{3,4},{4,5},{5,6},{6,7},{8,9},{9,10},{10,11},{11... | collective-permute-start | bytes 36872 | tf_op jit(solution)/shard_map/ppermute | solution.py:15
  89.3 12.1 %copy-start.3 = (f32[2,4096]{1,0:T(2,128)S(1)}, f32[2,4096]{1,0:T(2,128)}, u32[]{:S(2)}) copy-start(f32[2,4096]{1,0:T(2,128)} %param.22) | copy-start | bytes 98308
  100.1 15.9 %collective-permute-start.1 = (f32[3,1024]{0,1:T(8,128)S(1)}, f32[3,1024]{0,1:T(8,128)S(1)}, u32[]{:S(2)}, u32[]{:S(2)}) collective-permute-start(f32[3,1024]{0,1:T(8,128)S(1)} %get-tuple-element.80), channel_id=1, source_target_pairs={{1,0},{2,1},{3,2},{4,3},{5,4},{6,5},{7,6},{9,8},{10,9},{11,10},{12... | collective-permute-start | bytes 36872 | tf_op jit(solution)/shard_map/ppermute | solution.py:15
  167.2 37.4 %copy-start.2 = (f32[2048]{0:T(1024)S(1)}, f32[2048]{0:T(1024)}, u32[]{:S(2)}) copy-start(f32[2048]{0:T(1024)} %param.23) | copy-start | bytes 24580
  200.3 15.9 %collective-permute-start.2 = (f32[3,1024]{0,1:T(8,128)S(1)}, f32[3,1024]{0,1:T(8,128)S(1)}, u32[]{:S(2)}, u32[]{:S(2)}) collective-permute-start(f32[3,1024]{0,1:T(8,128)S(1)} %slice.292), channel_id=1, source_target_pairs={{0,1},{1,2},{2,3},{3,4},{4,5},{5,6},{6,7},{8,9},{9,10},{10,11},{11... | collective-permute-start | bytes 36872 | tf_op jit(solution)/shard_map/ppermute | solution.py:15
  242.3 19.3 %copy-start.1 = (f32[3,2048]{0,1:T(8,128)}, f32[3,2048]{0,1:T(8,128)S(1)}, u32[]{:S(2)}) copy-start(f32[3,2048]{0,1:T(8,128)S(1)} %get-tuple-element.76) | copy-start | bytes 73732
  261.7 11.4 %collective-permute-start.3 = (f32[3,1024]{0,1:T(8,128)S(1)}, f32[3,1024]{0,1:T(8,128)S(1)}, u32[]{:S(2)}, u32[]{:S(2)}) collective-permute-start(f32[3,1024]{0,1:T(8,128)S(1)} %slice.293), channel_id=1, source_target_pairs={{1,0},{2,1},{3,2},{4,3},{5,4},{6,5},{7,6},{9,8},{10,9},{11,10},{12... | collective-permute-start | bytes 36872 | tf_op jit(solution)/shard_map/ppermute | solution.py:15
  367.0 16.4 %collective-permute-start.4 = (f32[3,1024]{0,1:T(8,128)S(1)}, f32[3,1024]{0,1:T(8,128)S(1)}, u32[]{:S(2)}, u32[]{:S(2)}) collective-permute-start(f32[3,1024]{0,1:T(8,128)S(1)} %slice.299), channel_id=1, source_target_pairs={{0,1},{1,2},{2,3},{3,4},{4,5},{5,6},{6,7},{8,9},{9,10},{10,11},{11... | collective-permute-start | bytes 36872 | tf_op jit(solution)/shard_map/ppermute | solution.py:15
  384.2 24.7 %copy-start = (f32[3,2048]{0,1:T(8,128)}, f32[3,2048]{0,1:T(8,128)S(1)}, u32[]{:S(2)}) copy-start(f32[3,2048]{0,1:T(8,128)S(1)} %fusion.9) | copy-start | bytes 73732
  429.7 11.1 %collective-permute-start.5 = (f32[3,1024]{0,1:T(8,128)S(1)}, f32[3,1024]{0,1:T(8,128)S(1)}, u32[]{:S(2)}, u32[]{:S(2)}) collective-permute-start(f32[3,1024]{0,1:T(8,128)S(1)} %slice.300), channel_id=1, source_target_pairs={{1,0},{2,1},{3,2},{4,3},{5,4},{6,5},{7,6},{9,8},{10,9},{11,10},{12... | collective-permute-start | bytes 36872 | tf_op jit(solution)/shard_map/ppermute | solution.py:15
  547.9 16.3 %collective-permute-start.6 = (f32[3,1024]{0,1:T(8,128)S(1)}, f32[3,1024]{0,1:T(8,128)S(1)}, u32[]{:S(2)}, u32[]{:S(2)}) collective-permute-start(f32[3,1024]{0,1:T(8,128)S(1)} %slice.306), channel_id=1, source_target_pairs={{0,1},{1,2},{2,3},{3,4},{4,5},{5,6},{6,7},{8,9},{9,10},{10,11},{11... | collective-permute-start | bytes 36872 | tf_op jit(solution)/shard_map/ppermute | solution.py:15
  587.6 11.3 %collective-permute-start.7 = (f32[3,1024]{0,1:T(8,128)S(1)}, f32[3,1024]{0,1:T(8,128)S(1)}, u32[]{:S(2)}, u32[]{:S(2)}) collective-permute-start(f32[3,1024]{0,1:T(8,128)S(1)} %slice.307), channel_id=1, source_target_pairs={{1,0},{2,1},{3,2},{4,3},{5,4},{6,5},{7,6},{9,8},{10,9},{11,10},{12... | collective-permute-start | bytes 36872 | tf_op jit(solution)/shard_map/ppermute | solution.py:15
where the time goes:
time: 643 us; the launch traced here: 632 us
  blocking collectives  230 us (36%)
  other arithmetic  178 us (28%)
  local copies, waits for them, and re-layouts  111 us (17%)
  waiting for transfers between devices  83.3 us (13%)
  starting transfers between devices  22.8 us (4%)
  between operations  7.44 us (1%)
    psum x3, blocking collectives, body(): forces = lax.psum(forces, 'grp')  97.6 us
    scatter-add x12, other arithmetic, element_forces(): forces = forces.at[:, connect[corner]].add(nodal)  92.3 us
    ppermute x8, waiting for transfers between devices, shifted(): return lax.ppermute(shard, axis, pairs)  83.3 us
    psum x3, blocking collectives, squares(): return lax.psum(jnp.sum(residual * residual), 'sub')  57.7 us
    gather x12, local copies, waits for them, and re-layouts, element_forces(): moved = jnp.take(field, connect[corner], axis=1)  56.8 us
    scatter-add x2, other arithmetic, body(): partial_rhs = jnp.zeros((3, span), jnp.float32).at[:, local_map[0]].add(h...  46.2 us
    psum x2, blocking collectives, body(): alpha = norm_now / lax.psum(curv, 'sub')  40.5 us
    psum x1, blocking collectives, body(): column_rhs = lax.psum(partial_rhs, 'grp')  34.5 us
  transfers between devices with their start and end apart: 8, of which 8 were waited for; matrix products, arithmetic and copies ran while one was open for 1% of the time, Pallas kernels for 0%

commit v1 on v0

--- a/solution.py
+++ b/solution.py
@@ -56,7 +56,7 @@
         .at[:, local_map[1]]
         .add(half)
     )
-    column_rhs = lax.psum(partial_rhs, "grp")
+    column_rhs = jnp.sum(lax.all_gather(partial_rhs, "grp"), axis=0)
     carried = shifted(column_rhs[:, CN:], "sub", 1)
     rhs = column_rhs[:, :CN].at[:, :CI].add(carried)
     solution = jnp.zeros(rhs.shape, jnp.float32)

time: 643 us -> 617 us (0.960)
  blocking collectives: 230 us -> 203 us
    psum x1 -> x0, blocking collectives: 34.5 us -> none  [body(): column_rhs = lax.psum(partial_rhs, 'grp')]
    all_gather x0 -> x1, blocking collectives: none -> 6.86 us  [body(): column_rhs = jnp.sum(lax.all_gather(partial_rhs, 'grp'), axis=0)]
where the time goes in v1:
time: 617 us; the launch traced here: 607 us
  blocking collectives  203 us (33%)
  other arithmetic  178 us (29%)
  local copies, waits for them, and re-layouts  113 us (18%)
  waiting for transfers between devices  83.2 us (13%)
  starting transfers between devices  23.2 us (4%)
  between operations  7.47 us (1%)
    psum x3, blocking collectives, body(): forces = lax.psum(forces, 'grp')  97.8 us
    scatter-add x12, other arithmetic, element_forces(): forces = forces.at[:, connect[corner]].add(nodal)  92.3 us
    ppermute x8, waiting for transfers between devices, shifted(): return lax.ppermute(shard, axis, pairs)  83.2 us
    psum x3, blocking collectives, squares(): return lax.psum(jnp.sum(residual * residual), 'sub')  57.6 us
    gather x12, local copies, waits for them, and re-layouts, element_forces(): moved = jnp.take(field, connect[corner], axis=1)  56.8 us
    scatter-add x2, other arithmetic, body(): partial_rhs = jnp.zeros((3, span), jnp.float32).at[:, local_map[0]].add(h...  46.3 us
    psum x2, blocking collectives, body(): alpha = norm_now / lax.psum(curv, 'sub')  40.5 us
    ppermute x8, starting transfers between devices, shifted(): return lax.ppermute(shard, axis, pairs)  23.2 us
  transfers between devices with their start and end apart: 8, of which 8 were waited for; matrix products, arithmetic and copies ran while one was open for 1% of the time, Pallas kernels for 0%

profile of v1, /device:TPU:0, one launch (start us, length us, event | category | flops | bytes accessed | tf_op | source)
XLA Modules:
  0.0 607.3 jit_solution(5054294759038939380)
XLA Ops:
  3.7 23.0 %scatter_custom_fusion = f32[3,3072]{0,1:T(8,128)S(1)} fusion(s32[4096]{0:T(1024)S(1)} %bitcast.141, f32[4096,3]{1,0:T(8,128)} %copy.215, f32[]{:T(128)} %constant.127.clone.1), kind=kCustom, calls=%fused_computation.56 | custom fusion | flops 12288 | bytes 37376 | tf_op jit(solution)/shard_map/scatter-add | solution.py:55
  26.7 23.3 %scatter_fusion = f32[3,3072]{0,1:T(8,128)S(1)} fusion(f32[3,3072]{0,1:T(8,128)S(1)} %scatter_custom_fusion, s32[4096]{0:T(1024)S(1)} %bitcast.114, f32[4096,3]{1,0:T(8,128)} %copy.215), kind=kCustom, calls=%fused_computation.15 | custom fusion | flops 12288 | bytes 163840 | tf_op jit(solution)/shard_map/scatter-add | solution.py:57
  50.5 6.9 %all-gather.1 = f32[4,3,3072]{2,1,0:T(4,128)S(1)} all-gather(f32[1,3,3072]{2,1,0:T(4,128)S(1)} %copy.217), channel_id=2, replica_groups=mesh['grp'=4,'sub'=8] {'grp'}, dimensions={0}, use_global_device_ids=true | all-gather | bytes 184320 | tf_op jit(solution)/shard_map/all_gather | solution.py:59
  64.5 8.5 %collective-permute-done = f32[3,1024]{0,1:T(8,128)S(1)} collective-permute-done((f32[3,1024]{0,1:T(8,128)S(1)}, f32[3,1024]{0,1:T(8,128)S(1)}, u32[]{:S(2)}, u32[]{:S(2)}) %collective-permute-start) | collective-permute-done | bytes 12320 | tf_op jit(solution)/shard_map/ppermute | solution.py:15
  75.1 14.5 %collective-permute-done.1 = f32[3,1024]{0,1:T(8,128)S(1)} collective-permute-done((f32[3,1024]{0,1:T(8,128)S(1)}, f32[3,1024]{0,1:T(8,128)S(1)}, u32[]{:S(2)}, u32[]{:S(2)}) %collective-permute-start.1) | collective-permute-done | bytes 12320 | tf_op jit(solution)/shard_map/ppermute | solution.py:15
  112.9 6.8 %scatter_custom_fusion.2 = f32[3,3072]{0,1:T(8,128)S(1)} fusion(s32[1024]{0:T(1024)S(1)} %bitcast.142, f32[1024,3]{1,0:T(8,128)} %copy.231, f32[]{:T(128)} %constant.127.clone.1), kind=kCustom, calls=%fused_computation.54 | custom fusion | flops 3072 | bytes 37376 | tf_op jit(solution)/shard_map/scatter-add | solution.py:32
  119.7 7.5 %scatter_fusion.1 = f32[3,3072]{0,1:T(8,128)S(1)} fusion(f32[3,3072]{0,1:T(8,128)S(1)} %scatter_custom_fusion.2, s32[1024]{0:T(1024)S(1)} %bitcast.111, f32[1024,3]{1,0:T(8,128)} %copy.232), kind=kCustom, calls=%fused_computation.17 | custom fusion | flops 3072 | bytes 40960 | tf_op jit(solution)/shard_map/scatter-add | solution.py:32
  127.2 7.0 %scatter_fusion.2 = f32[3,3072]{0,1:T(8,128)S(1)} fusion(f32[3,3072]{0,1:T(8,128)S(1)} %scatter_fusion.1, s32[1024]{0:T(1024)S(1)} %bitcast.108, f32[1024,3]{1,0:T(8,128)} %copy.233), kind=kCustom, calls=%fused_computation.18 | custom fusion | flops 3072 | bytes 40960 | tf_op jit(solution)/shard_map/scatter-add | solution.py:32
  140.9 32.6 %psum.64 = f32[3,3072]{0,1:T(8,128)} all-reduce(f32[3,3072]{0,1:T(8,128)S(1)} %scatter_fusion.3), channel_id=1, replica_groups=mesh['grp'=4,'sub'=8] {'grp'}, use_global_device_ids=true, to_apply=%region_14.16 | all-reduce | flops 9216 | bytes 73728 | tf_op jit(solution)/shard_map/psum | solution.py:70
  180.7 9.8 %collective-permute-done.2 = f32[3,1024]{0,1:T(8,128)S(1)} collective-permute-done((f32[3,1024]{0,1:T(8,128)S(1)}, f32[3,1024]{0,1:T(8,128)S(1)}, u32[]{:S(2)}, u32[]{:S(2)}) %collective-permute-start.2) | collective-permute-done | bytes 12320 | tf_op jit(solution)/shard_map/ppermute | solution.py:15
  192.2 22.1 %all-reduce = (f32[]{:T(128)}, f32[]{:T(128)}) all-reduce(f32[]{:T(128)} %get-tuple-element.56, f32[]{:T(128)} %get-tuple-element.55), channel_id=1, replica_groups=mesh['grp'=4,'sub'=8] {'sub'}, use_global_device_ids=true, to_apply=%region_5.0 | all-reduce | flops 2 | bytes 16 | tf_op jit(solution)/shard_map/psum | solution.py:37
  216.6 17.9 %psum.66 = f32[]{:T(128)} all-reduce(f32[]{:T(128)} %get-tuple-element.75), channel_id=1, replica_groups=mesh['grp'=4,'sub'=8] {'sub'}, use_global_device_ids=true, to_apply=%region_18.20 | all-reduce | flops 1 | bytes 8 | tf_op jit(solution)/shard_map/psum | solution.py:37
  237.3 10.1 %collective-permute-done.3 = f32[3,1024]{0,1:T(8,128)S(1)} collective-permute-done((f32[3,1024]{0,1:T(8,128)S(1)}, f32[3,1024]{0,1:T(8,128)S(1)}, u32[]{:S(2)}, u32[]{:S(2)}) %collective-permute-start.3) | collective-permute-done | bytes 12320 | tf_op jit(solution)/shard_map/ppermute | solution.py:15
  274.3 7.4 %scatter_custom_fusion.6 = f32[3,3072]{0,1:T(8,128)} fusion(s32[1024]{0:T(1024)S(1)} %bitcast.143, f32[1024,3]{1,0:T(8,128)S(1)} %copy.243, f32[]{:T(128)} %constant.127.clone.1), kind=kCustom, calls=%fused_computation.52 | custom fusion | flops 3072 | bytes 36868 | tf_op jit(solution)/shard_map/scatter-add | solution.py:32
  283.2 8.0 %scatter_fusion.4 = f32[3,3072]{0,1:T(8,128)} fusion(f32[3,3072]{0,1:T(8,128)} %scatter_custom_fusion.6, s32[1024]{0:T(1024)S(1)} %bitcast.112, f32[1024,3]{1,0:T(8,128)S(1)} %copy.244), kind=kCustom, calls=%fused_computation.21 | custom fusion | flops 3072 | bytes 40960 | tf_op jit(solution)/shard_map/scatter-add | solution.py:32
  291.1 8.0 %scatter_fusion.5 = f32[3,3072]{0,1:T(8,128)} fusion(f32[3,3072]{0,1:T(8,128)} %scatter_fusion.4, s32[1024]{0:T(1024)S(1)} %bitcast.109, f32[1024,3]{1,0:T(8,128)S(1)} %copy.245), kind=kCustom, calls=%fused_computation.22 | custom fusion | flops 3072 | bytes 40960 | tf_op jit(solution)/shard_map/scatter-add | solution.py:32
  299.1 8.4 %scatter_fusion.6 = f32[3,3072]{0,1:T(8,128)} fusion(f32[3,3072]{0,1:T(8,128)} %scatter_fusion.5, s32[1024]{0:T(1024)S(1)} %bitcast.106, f32[1024,3]{1,0:T(8,128)} %copy.246), kind=kCustom, calls=%fused_computation.23 | custom fusion | flops 3072 | bytes 40960 | tf_op jit(solution)/shard_map/scatter-add | solution.py:32
  307.5 32.5 %psum.67 = f32[3,3072]{0,1:T(8,128)} all-reduce(f32[3,3072]{0,1:T(8,128)} %scatter_fusion.6), channel_id=1, replica_groups=mesh['grp'=4,'sub'=8] {'grp'}, use_global_device_ids=true, to_apply=%region_27.29 | all-reduce | flops 9216 | bytes 73728 | tf_op jit(solution)/shard_map/psum | solution.py:70
  347.5 10.2 %collective-permute-done.4 = f32[3,1024]{0,1:T(8,128)S(1)} collective-permute-done((f32[3,1024]{0,1:T(8,128)S(1)}, f32[3,1024]{0,1:T(8,128)S(1)}, u32[]{:S(2)}, u32[]{:S(2)}) %collective-permute-start.4) | collective-permute-done | bytes 12320 | tf_op jit(solution)/shard_map/ppermute | solution.py:15
  359.5 20.3 %psum.68 = f32[]{:T(128)} all-reduce(f32[]{:T(128)} %multiply_reduce_fusion.2), channel_id=1, replica_groups=mesh['grp'=4,'sub'=8] {'sub'}, use_global_device_ids=true, to_apply=%region_29.31 | all-reduce | flops 1 | bytes 8 | tf_op jit(solution)/shard_map/psum | solution.py:75
  383.3 17.7 %psum.69 = f32[]{:T(128)} all-reduce(f32[]{:T(128)} %multiply_reduce_fusion.1), channel_id=1, replica_groups=mesh['grp'=4,'sub'=8] {'sub'}, use_global_device_ids=true, to_apply=%region_31.33 | all-reduce | flops 1 | bytes 8 | tf_op jit(solution)/shard_map/psum | solution.py:37
  405.5 9.5 %collective-permute-done.5 = f32[3,1024]{0,1:T(8,128)S(1)} collective-permute-done((f32[3,1024]{0,1:T(8,128)S(1)}, f32[3,1024]{0,1:T(8,128)S(1)}, u32[]{:S(2)}, u32[]{:S(2)}) %collective-permute-start.5) | collective-permute-done | bytes 12320 | tf_op jit(solution)/shard_map/ppermute | solution.py:15
  452.3 7.6 %scatter_custom_fusion.10 = f32[3,3072]{0,1:T(8,128)} fusion(s32[1024]{0:T(1024)S(1)} %bitcast.144, f32[1024,3]{1,0:T(8,128)} %copy.255, f32[]{:T(128)} %constant.127.clone.1), kind=kCustom, calls=%fused_computation.50 | custom fusion | flops 3072 | bytes 37376 | tf_op jit(solution)/shard_map/scatter-add | solution.py:32
  463.1 8.4 %scatter_fusion.7 = f32[3,3072]{0,1:T(8,128)} fusion(f32[3,3072]{0,1:T(8,128)} %scatter_custom_fusion.10, s32[1024]{0:T(1024)S(1)} %bitcast.113, f32[1024,3]{1,0:T(8,128)} %copy.256), kind=kCustom, calls=%fused_computation.25 | custom fusion | flops 3072 | bytes 40960 | tf_op jit(solution)/shard_map/scatter-add | solution.py:32
  471.4 8.4 %scatter_fusion.8 = f32[3,3072]{0,1:T(8,128)} fusion(f32[3,3072]{0,1:T(8,128)} %scatter_fusion.7, s32[1024]{0:T(1024)S(1)} %bitcast.110, f32[1024,3]{1,0:T(8,128)} %copy.257), kind=kCustom, calls=%fused_computation.26 | custom fusion | flops 3072 | bytes 40960 | tf_op jit(solution)/shard_map/scatter-add | solution.py:32
  479.8 8.4 %scatter_fusion.9 = f32[3,3072]{0,1:T(8,128)} fusion(f32[3,3072]{0,1:T(8,128)} %scatter_fusion.8, s32[1024]{0:T(1024)S(1)} %bitcast.107, f32[1024,3]{1,0:T(8,128)} %copy.258), kind=kCustom, calls=%fused_computation.27 | custom fusion | flops 3072 | bytes 40960 | tf_op jit(solution)/shard_map/scatter-add | solution.py:32
  488.2 32.7 %psum.70 = f32[3,3072]{0,1:T(8,128)} all-reduce(f32[3,3072]{0,1:T(8,128)} %scatter_fusion.9), channel_id=1, replica_groups=mesh['grp'=4,'sub'=8] {'grp'}, use_global_device_ids=true, to_apply=%region_40.42 | all-reduce | flops 9216 | bytes 73728 | tf_op jit(solution)/shard_map/psum | solution.py:70
  528.3 10.1 %collective-permute-done.6 = f32[3,1024]{0,1:T(8,128)S(1)} collective-permute-done((f32[3,1024]{0,1:T(8,128)S(1)}, f32[3,1024]{0,1:T(8,128)S(1)}, u32[]{:S(2)}, u32[]{:S(2)}) %collective-permute-start.6) | collective-permute-done | bytes 12320 | tf_op jit(solution)/shard_map/ppermute | solution.py:15
  540.1 20.2 %psum.71 = f32[]{:T(128)} all-reduce(f32[]{:T(128)} %multiply_reduce_fusion), channel_id=1, replica_groups=mesh['grp'=4,'sub'=8] {'sub'}, use_global_device_ids=true, to_apply=%region_42.44 | all-reduce | flops 1 | bytes 8 | tf_op jit(solution)/shard_map/psum | solution.py:75
  563.2 10.5 %collective-permute-done.7 = f32[3,1024]{0,1:T(8,128)S(1)} collective-permute-done((f32[3,1024]{0,1:T(8,128)S(1)}, f32[3,1024]{0,1:T(8,128)S(1)}, u32[]{:S(2)}, u32[]{:S(2)}) %collective-permute-start.7) | collective-permute-done | bytes 12320 | tf_op jit(solution)/shard_map/ppermute | solution.py:15
  573.8 14.1 %gather_fusion.12 = f32[4096,3]{1,0:T(8,128)} fusion(f32[3,3072]{0,1:T(8,128)S(1)} %pad_maximum_fusion.3, s32[4096]{0:T(1024)S(1)} %fusion.12), kind=kCustom, calls=%fused_computation.1.clone | custom fusion | bytes 114688 | tf_op jit(solution)/shard_map/jit(_take)/gather | solution.py:85
  590.0 14.1 %gather_fusion.13 = f32[4096,3]{1,0:T(8,128)} fusion(f32[3,3072]{0,1:T(8,128)S(1)} %pad_maximum_fusion.3, s32[4096]{0:T(1024)S(1)} %fusion.13), kind=kCustom, calls=%fused_computation.13.clone | custom fusion | bytes 114688 | tf_op jit(solution)/shard_map/jit(_take)/gather | solution.py:85
  (131 shorter events, 153.6 us)
Async XLA Ops:
  57.6 15.3 %collective-permute-start = (f32[3,1024]{0,1:T(8,128)S(1)}, f32[3,1024]{0,1:T(8,128)S(1)}, u32[]{:S(2)}, u32[]{:S(2)}) collective-permute-start(f32[3,1024]{0,1:T(8,128)S(1)} %copy.218), channel_id=1, source_target_pairs={{0,1},{1,2},{2,3},{3,4},{4,5},{5,6},{6,7},{8,9},{9,10},{10,11},{11... | collective-permute-start | bytes 36872 | tf_op jit(solution)/shard_map/ppermute | solution.py:15
  63.5 11.5 %copy-start.3 = (f32[2,4096]{1,0:T(2,128)S(1)}, f32[2,4096]{1,0:T(2,128)}, u32[]{:S(2)}) copy-start(f32[2,4096]{1,0:T(2,128)} %param.22) | copy-start | bytes 98308
  73.7 16.0 %collective-permute-start.1 = (f32[3,1024]{0,1:T(8,128)S(1)}, f32[3,1024]{0,1:T(8,128)S(1)}, u32[]{:S(2)}, u32[]{:S(2)}) collective-permute-start(f32[3,1024]{0,1:T(8,128)S(1)} %get-tuple-element.80), channel_id=1, source_target_pairs={{1,0},{2,1},{3,2},{4,3},{5,4},{6,5},{7,6},{9,8},{10,9},{11,10},{12... | collective-permute-start | bytes 36872 | tf_op jit(solution)/shard_map/ppermute | solution.py:15
  140.9 38.2 %copy-start.2 = (f32[2048]{0:T(1024)S(1)}, f32[2048]{0:T(1024)}, u32[]{:S(2)}) copy-start(f32[2048]{0:T(1024)} %param.23) | copy-start | bytes 24580
  174.5 16.0 %collective-permute-start.2 = (f32[3,1024]{0,1:T(8,128)S(1)}, f32[3,1024]{0,1:T(8,128)S(1)}, u32[]{:S(2)}, u32[]{:S(2)}) collective-permute-start(f32[3,1024]{0,1:T(8,128)S(1)} %slice.292), channel_id=1, source_target_pairs={{0,1},{1,2},{2,3},{3,4},{4,5},{5,6},{6,7},{8,9},{9,10},{10,11},{11... | collective-permute-start | bytes 36872 | tf_op jit(solution)/shard_map/ppermute | solution.py:15
  216.6 19.3 %copy-start.1 = (f32[3,2048]{0,1:T(8,128)}, f32[3,2048]{0,1:T(8,128)S(1)}, u32[]{:S(2)}) copy-start(f32[3,2048]{0,1:T(8,128)S(1)} %get-tuple-element.76) | copy-start | bytes 73732
  236.0 11.4 %collective-permute-start.3 = (f32[3,1024]{0,1:T(8,128)S(1)}, f32[3,1024]{0,1:T(8,128)S(1)}, u32[]{:S(2)}, u32[]{:S(2)}) collective-permute-start(f32[3,1024]{0,1:T(8,128)S(1)} %slice.293), channel_id=1, source_target_pairs={{1,0},{2,1},{3,2},{4,3},{5,4},{6,5},{7,6},{9,8},{10,9},{11,10},{12... | collective-permute-start | bytes 36872 | tf_op jit(solution)/shard_map/ppermute | solution.py:15
  341.1 16.6 %collective-permute-start.4 = (f32[3,1024]{0,1:T(8,128)S(1)}, f32[3,1024]{0,1:T(8,128)S(1)}, u32[]{:S(2)}, u32[]{:S(2)}) collective-permute-start(f32[3,1024]{0,1:T(8,128)S(1)} %slice.299), channel_id=1, source_target_pairs={{0,1},{1,2},{2,3},{3,4},{4,5},{5,6},{6,7},{8,9},{9,10},{10,11},{11... | collective-permute-start | bytes 36872 | tf_op jit(solution)/shard_map/ppermute | solution.py:15
  358.5 24.7 %copy-start = (f32[3,2048]{0,1:T(8,128)}, f32[3,2048]{0,1:T(8,128)S(1)}, u32[]{:S(2)}) copy-start(f32[3,2048]{0,1:T(8,128)S(1)} %fusion.9) | copy-start | bytes 73732
  403.9 11.1 %collective-permute-start.5 = (f32[3,1024]{0,1:T(8,128)S(1)}, f32[3,1024]{0,1:T(8,128)S(1)}, u32[]{:S(2)}, u32[]{:S(2)}) collective-permute-start(f32[3,1024]{0,1:T(8,128)S(1)} %slice.300), channel_id=1, source_target_pairs={{1,0},{2,1},{3,2},{4,3},{5,4},{6,5},{7,6},{9,8},{10,9},{11,10},{12... | collective-permute-start | bytes 36872 | tf_op jit(solution)/shard_map/ppermute | solution.py:15
  521.9 16.4 %collective-permute-start.6 = (f32[3,1024]{0,1:T(8,128)S(1)}, f32[3,1024]{0,1:T(8,128)S(1)}, u32[]{:S(2)}, u32[]{:S(2)}) collective-permute-start(f32[3,1024]{0,1:T(8,128)S(1)} %slice.306), channel_id=1, source_target_pairs={{0,1},{1,2},{2,3},{3,4},{4,5},{5,6},{6,7},{8,9},{9,10},{10,11},{11... | collective-permute-start | bytes 36872 | tf_op jit(solution)/shard_map/ppermute | solution.py:15
  561.8 11.8 %collective-permute-start.7 = (f32[3,1024]{0,1:T(8,128)S(1)}, f32[3,1024]{0,1:T(8,128)S(1)}, u32[]{:S(2)}, u32[]{:S(2)}) collective-permute-start(f32[3,1024]{0,1:T(8,128)S(1)} %slice.307), channel_id=1, source_target_pairs={{1,0},{2,1},{3,2},{4,3},{5,4},{6,5},{7,6},{9,8},{10,9},{11,10},{12... | collective-permute-start | bytes 36872 | tf_op jit(solution)/shard_map/ppermute | solution.py:15
